TPU v7x, 32 devices: a whole 2x2x4 slice. The times are simulated.
32 devices in a mesh: dp: 4 (over x, core), expert: 8 (over z, y).
Axes of the slice: x: 2, y: 2, z: 4, core: 2. Of those that a mesh axis runs over, the one named last changes fastest.
Arguments:
- tokens: bfloat16 [1024, 6144], P('dp', 'expert'), may hold values from -6 to 6
- cotangent: bfloat16 [1024, 6144], P('dp', 'expert'), may hold values from -6 to 6
- expert_choice: int32 [1024, 2], P('dp'), may hold values from 0 to 3, all different within a row; in each aligned block of 256 rows (0 to 255, 256 to 511, ...) at most 160 rows name the same one
- gate_values: bfloat16 [1024, 2], P('dp'), may hold values from 0.099609375 to 1
- gate_weight: bfloat16 [4, 6144, 2048], P('dp', None, 'expert'), may hold values from -0.078125 to 0.078125
- up_weight: bfloat16 [4, 6144, 2048], P('dp', None, 'expert'), may hold values from -0.078125 to 0.078125
- down_weight: bfloat16 [4, 2048, 6144], P('dp', 'expert'), may hold values from -0.125 to 0.125
- shrinker: bfloat16 [4, 32, 6144], P('dp'), may hold values from -0.078125 to 0.078125
- widener: bfloat16 [4, 2, 16, 2048], P('dp', None, None, 'expert'), may hold values from -0.375 to 0.375
- squeezer: bfloat16 [4, 16, 2048], P('dp', None, 'expert'), may hold values from -0.125 to 0.125
- spreader: bfloat16 [4, 16, 6144], P('dp'), may hold values from -0.375 to 0.375
Outputs:
- token_grad: bfloat16 [1024, 6144], P('dp', 'expert')
- gate_grad: float32 [1024, 2], P('dp')
- shrinker_grad: float32 [4, 32, 6144], P('dp')
- widener_grad: float32 [4, 2, 16, 2048], P('dp', None, None, 'expert')
- squeezer_grad: float32 [4, 16, 2048], P('dp', None, 'expert')
- spreader_grad: float32 [4, 16, 6144], P('dp')
Inputs may be any that keep to these rules, and one draw needn't show every extreme that they name: `expert_choice`: each row names 2 different experts. Among the 256 tokens of one index of dp no expert is chosen more than 160 times, and some expert is chosen exactly 160 times by the tokens of some or all indices of dp.
All inputs are finite; a program needn't handle non-finite values.
Results may differ from a plain program's by a relative error of at most 0.02.
Values may be sent and summed in bfloat16 or wider, within the bound.
A program may use at most 128 MiB of HBM per device.

v0:
```python
import jax
import jax.numpy as jnp
from jax import lax
from jax.sharding import PartitionSpec as P

adapter_scale = 2.0


def product(pattern, operand_a, operand_b):
    return jnp.einsum(pattern, operand_a, operand_b, preferred_element_type=jnp.float32)


def silu_pair(gate_pre):
    logistic = jax.nn.sigmoid(gate_pre)
    return (gate_pre * logistic, logistic * (1.0 + gate_pre * (1.0 - logistic)))


def full_rows(gathered, capacity, part_width):
    n_groups = gathered.shape[0]
    n_sources = gathered.shape[1]
    ordered = gathered.reshape(n_groups, n_sources, capacity, part_width).transpose(1, 2, 0, 3)
    return ordered.reshape(n_sources * capacity, n_groups * part_width)


def local(
    tokens,
    cotangent,
    expert_choice,
    gate_values,
    gate_weight,
    up_weight,
    down_weight,
    shrinker,
    widener,
    squeezer,
    spreader,
):
    tok_rows, part_width = tokens.shape
    top_k = expert_choice.shape[1]
    low_rank = spreader.shape[1]
    n_groups = lax.axis_size("expert")
    n_experts = lax.axis_size("dp")
    capacity = tok_rows * top_k * 5 // (4 * n_experts)
    own_rows = n_experts * capacity
    flat_choice = expert_choice.reshape(-1)
    onehot = (flat_choice[:, None] == jnp.arange(n_experts, dtype=jnp.int32)[None, :]).astype(
        jnp.int32
    )
    before = jnp.cumsum(onehot, axis=0) - onehot
    slot_index = jnp.sum(before * onehot, axis=1)
    target = flat_choice * capacity + slot_index
    placing = target[None, :] == jnp.arange(own_rows, dtype=jnp.int32)[:, None]
    stacked = jnp.repeat(jnp.concatenate([tokens, cotangent], axis=1), top_k, axis=0)
    placed = jnp.dot(
        placing.astype(jnp.bfloat16), stacked, preferred_element_type=jnp.float32
    ).astype(jnp.bfloat16)
    send_x = placed[:, :part_width].reshape(n_experts, capacity * part_width)
    send_dy = placed[:, part_width:].reshape(n_experts, capacity * part_width)
    gate_flat = gate_values.reshape(-1).astype(jnp.float32)
    send_gate = (
        jnp.sum(jnp.where(placing, gate_flat[None, :], 0.0), axis=1)
        .astype(jnp.bfloat16)
        .reshape(n_experts, capacity)
    )
    recv_x, recv_dy, recv_gate = (
        lax.all_to_all(send_x, "dp", split_axis=0, concat_axis=0, tiled=True),
        lax.all_to_all(send_dy, "dp", split_axis=0, concat_axis=0, tiled=True),
        lax.all_to_all(send_gate, "dp", split_axis=0, concat_axis=0, tiled=True),
    )
    gate_rows = recv_gate.reshape(-1).astype(jnp.float32)
    gathered_x = lax.all_gather(recv_x[None], "expert", axis=0, tiled=True)
    rows_x = full_rows(gathered_x, capacity, part_width)
    shrink_local = shrinker[0]
    widen_local = widener[0]
    squeeze_local = squeezer[0]
    spread_local = spreader[0]
    lowrank_in = product("nd,rd->nr", rows_x, shrink_local).astype(jnp.bfloat16)
    gate_pre = jnp.dot(
        rows_x, gate_weight[0], preferred_element_type=jnp.float32
    ) + adapter_scale * jnp.dot(
        lowrank_in[:, :low_rank], widen_local[0], preferred_element_type=jnp.float32
    )
    up_pre = jnp.dot(
        rows_x, up_weight[0], preferred_element_type=jnp.float32
    ) + adapter_scale * jnp.dot(
        lowrank_in[:, low_rank:], widen_local[1], preferred_element_type=jnp.float32
    )
    silu_gate, silu_slope = silu_pair(gate_pre)
    activation = (silu_gate * up_pre).astype(jnp.bfloat16)
    out_part = product("rf,nf->rn", squeeze_local, activation)
    out_low = lax.psum(out_part.astype(jnp.bfloat16), "expert").astype(jnp.float32)
    gathered_dy = lax.all_gather(recv_dy[None], "expert", axis=0, tiled=True)
    rows_dy = full_rows(gathered_dy, capacity, part_width)
    back_down = product("nd,fd->nf", rows_dy, down_weight[0])
    back_low = product("rd,nd->rn", spread_local, rows_dy)
    gate_part = jnp.sum(activation.astype(jnp.float32) * back_down, axis=1)
    scaled_low = (back_low * gate_rows[None, :]).astype(jnp.bfloat16)
    act_delta = gate_rows[:, None] * back_down + adapter_scale * product(
        "rn,rf->nf", scaled_low, squeeze_local
    )
    gate_delta = (act_delta * up_pre * silu_slope).astype(jnp.bfloat16)
    up_delta = (act_delta * silu_gate).astype(jnp.bfloat16)
    back_part = jnp.concatenate(
        [
            product("rf,nf->rn", widen_local[0], gate_delta),
            product("rf,nf->rn", widen_local[1], up_delta),
        ],
        axis=0,
    )
    back_sum, gate_sum = (
        lax.psum(back_part.astype(jnp.bfloat16), "expert").astype(jnp.float32),
        lax.psum(gate_part.astype(jnp.bfloat16), "expert").astype(jnp.float32),
    )
    low_out = out_low.astype(jnp.bfloat16)
    gate_dots = gate_sum + adapter_scale * jnp.sum(low_out.astype(jnp.float32) * back_low, axis=0)
    back_in = back_sum.astype(jnp.bfloat16)
    gate_blocks = gate_weight[0].reshape(n_groups, part_width, gate_weight.shape[2])
    up_blocks = up_weight[0].reshape(n_groups, part_width, up_weight.shape[2])
    term = product("nf,kdf->knd", gate_delta, gate_blocks) + product(
        "nf,kdf->knd", up_delta, up_blocks
    )
    token_part = (
        lax.psum_scatter(
            term.reshape(1 * lax.axis_size("expert"), own_rows * part_width).astype(jnp.bfloat16),
            "expert",
            scatter_dimension=0,
            tiled=True,
        )
        .astype(jnp.float32)
        .reshape(own_rows, part_width)
    )
    shrink_cols = lax.dynamic_slice_in_dim(
        shrink_local, lax.axis_index("expert") * part_width, part_width, 1
    )
    token_part = token_part + adapter_scale * product("rn,rd->nd", back_in, shrink_cols)
    token_back, gate_back = (
        lax.all_to_all(
            token_part.reshape(n_experts, capacity * part_width).astype(jnp.bfloat16),
            "dp",
            split_axis=0,
            concat_axis=0,
            tiled=True,
        ).astype(jnp.float32),
        lax.all_to_all(
            gate_dots.reshape(n_experts, capacity).astype(jnp.bfloat16),
            "dp",
            split_axis=0,
            concat_axis=0,
            tiled=True,
        ).astype(jnp.float32),
    )
    picked = jnp.take(token_back.reshape(own_rows, part_width), target, axis=0)
    token_grad = jnp.sum(picked.reshape(tok_rows, top_k, part_width), axis=1).astype(jnp.bfloat16)
    gate_grad = jnp.take(gate_back.reshape(own_rows), target).reshape(tok_rows, top_k)
    shrinker_grad = adapter_scale * product("rn,nd->rd", back_in, rows_x)
    widener_grad = adapter_scale * jnp.stack(
        [
            product("nr,nf->rf", lowrank_in[:, :low_rank], gate_delta),
            product("nr,nf->rf", lowrank_in[:, low_rank:], up_delta),
        ]
    )
    squeezer_grad = adapter_scale * product("rn,nf->rf", scaled_low, activation)
    weighted_low = (out_low * gate_rows[None, :]).astype(jnp.bfloat16)
    spreader_grad = adapter_scale * product("rn,nd->rd", weighted_low, rows_dy)
    return (
        token_grad,
        gate_grad,
        shrinker_grad[None],
        widener_grad[None],
        squeezer_grad[None],
        spreader_grad[None],
    )


def solution(mesh):
    placed = (
        P("dp", "expert"),
        P("dp", "expert"),
        P("dp", None),
        P("dp", None),
        P("dp", None, "expert"),
        P("dp", None, "expert"),
        P("dp", "expert", None),
        P("dp", None, None),
        P("dp", None, None, "expert"),
        P("dp", None, "expert"),
        P("dp", None, None),
    )
    return jax.shard_map(
        local,
        mesh=mesh,
        in_specs=placed,
        out_specs=(
            P("dp", "expert"),
            P("dp", None),
            P("dp", None, None),
            P("dp", None, None, "expert"),
            P("dp", None, "expert"),
            P("dp", None, None),
        ),
        check_vma=False,
    )
```

profile of v0, /device:TPU:0, one launch (start us, length us, event | category | flops | bytes accessed | tf_op | source)
XLA Modules:
  0.0 964.5 jit_solution(5538377547508068036)
XLA Ops:
  13.4 4.6 reshape.230
  26.2 9.3 reduce.14
  38.7 18.9 %all_to_all.38 = bf16[4,2,61440]{2,1,0:T(2,128)(2,1)} all-to-all(bf16[4,2,61440]{2,1,0:T(2,128)(2,1)} %reshape.284), channel_id=1, replica_groups=mesh['dp'=4,'expert'=8] {'dp'}, dimensions={0} | all-to-all | bytes 1966080 | tf_op jit(solution)/shard_map/all_to_all | solution.py:67
  65.3 9.3 reduce.15
  77.8 18.2 %all_to_all.39 = bf16[4,2,61440]{2,1,0:T(2,128)(2,1)} all-to-all(bf16[4,2,61440]{2,1,0:T(2,128)(2,1)} %reshape.282), channel_id=1, replica_groups=mesh['dp'=4,'expert'=8] {'dp'}, dimensions={0} | all-to-all | bytes 1966080 | tf_op jit(solution)/shard_map/all_to_all | solution.py:66
  100.6 6.1 all_to_all.40
  106.8 170.5 %all-gather.5.cloned.1.call-done = bf16[32,1,122880]{2,1,0:T(2,128)(2,1)} async-done(((bf16[4,1,122880]{2,1,0:T(2,128)(2,1)}), bf16[32,1,122880]{2,1,0:T(2,128)(2,1)}) %all-gather.5.cloned.1.call-update) | async-done | bytes 7864336 | tf_op jit(solution)/shard_map/all_gather | solution.py:92
  277.3 48.0 %reduce.2 = bf16[32,122880]{1,0:T(8,128)(2,1)} reduce(bf16[32,1,122880]{2,1,0:T(2,128)(2,1)} %all-gather.5.cloned.1.call-done, bf16[]{:T(256)} %constant.69), dimensions={1}, to_apply=%all-gather.reduce_sub_computation | reduce | bytes 15728642 | tf_op jit(solution)/shard_map/all_gather | solution.py:92
  325.3 8.2 copy.75
  333.5 10.9 %copy.60 = bf16[4,160,8,768]{3,2,1,0:T(8,128)(2,1)} copy(bf16[4,160,8,768]{3,1,0,2:T(8,128)(2,1)} %bitcast.132) | data formatting | bytes 15728640 | tf_op jit(solution)/shard_map/transpose | solution.py:21
  344.4 9.1 copy.76
  353.5 5.5 convolution_bitcast_fusion
  362.7 129.5 %all-gather.7.cloned.1.call-done = bf16[32,1,122880]{2,1,0:T(2,128)(2,1)} async-done(((bf16[4,1,122880]{2,1,0:T(2,128)(2,1)}), bf16[32,1,122880]{2,1,0:T(2,128)(2,1)}) %all-gather.7.cloned.1.call-update) | async-done | bytes 7864336 | tf_op jit(solution)/shard_map/all_gather | solution.py:71
  492.2 47.5 %reduce.3 = bf16[32,122880]{1,0:T(8,128)(2,1)} reduce(bf16[32,1,122880]{2,1,0:T(2,128)(2,1)} %all-gather.7.cloned.1.call-done, bf16[]{:T(256)} %constant.69), dimensions={1}, to_apply=%all-gather.1.reduce_sub_computation | reduce | bytes 15728642 | tf_op jit(solution)/shard_map/all_gather | solution.py:71
  539.6 8.2 copy.77
  547.9 10.8 %copy.63 = bf16[4,160,8,768]{3,2,1,0:T(8,128)(2,1)} copy(bf16[4,160,8,768]{3,1,0,2:T(8,128)(2,1)} %bitcast.134) | data formatting | bytes 15728640 | tf_op jit(solution)/shard_map/transpose | solution.py:21
  558.6 8.9 copy.78
  567.6 5.8 convolution_convert_fusion.1
  582.2 7.8 fusion.21
  590.0 11.1 %fusion.2 = bf16[1,8,640,768]{3,2,1,0:T(8,128)(2,1)} fusion(f32[640,8,768]{2,0,1:T(8,128)} %fusion.21, bf16[8,768,256]{2,1,0:T(8,128)(2,1)S(1)} %bitcast.136, bf16[640,256]{0,1:T(8,128)(2,1)S(1)} %get-tuple-element.40), kind=kOutput, calls=%fused_computation.7 | convolution fusion | flops 2021130240 | bytes 27066368 | tf_op jit(solution)/shard_map/nf,kdf->knd/dot_general | solution.py:10
  601.1 10.9 %copy.79 = bf16[1,8,640,768]{3,1,2,0:T(8,128)(2,1)} copy(bf16[1,8,640,768]{3,2,1,0:T(8,128)(2,1)} %fusion.2) | data formatting | bytes 15728640
  619.8 38.1 %all-reduce.1 = (bf16[32,640]{1,0:T(8,128)(2,1)S(1)}, bf16[16,640]{1,0:T(8,128)(2,1)S(1)}, bf16[640]{0:T(1024)(128)(2,1)}) all-reduce(bf16[32,640]{1,0:T(8,128)(2,1)} %pad_maximum_fusion.1, bf16[16,640]{1,0:T(8,128)(2,1)} %fusion.15, bf16[640]{0:T(1024)(128)(2,1)} %get-tuple-element.35), channel_id=1, replica_groups=mesh['dp'=4,'expert'=8] {'expert'}, use_global_device_ids=true, to_apply=%region_5.6 | all-reduce | flops 31360 | bytes 125440 | tf_op jit(solution)/shard_map/psum | solution.py:111
  669.2 5.7 fusion
  674.9 191.6 %all-reduce.4.cloned.1.call-done = bf16[8,491520]{1,0:T(8,128)(2,1)} async-done(((bf16[8,491520]{1,0:T(8,128)(2,1)}), bf16[8,491520]{1,0:T(8,128)(2,1)}) %all-reduce.4.cloned.1.call-update) | async-done | bytes 7864336
  866.5 21.8 %fusion.9 = f32[491520]{0:T(1024)} fusion(bf16[8,491520]{1,0:T(8,128)(2,1)} %all-reduce.4.cloned.1.call-done, u32[]{:T(128)} %bitcast.28), kind=kLoop, calls=%fused_computation.16 | loop fusion | flops 491520 | bytes 2949124 | tf_op jit(solution)/shard_map/reshape | solution.py:130
  897.8 9.3 reduce.16
  910.3 4.5 all-to-all-start.3
  914.8 5.1 fusion.1
  932.5 8.9 convert_reduce_fusion
  941.3 4.2 reshape.241
  945.5 4.7 gather_fusion
  953.3 4.2 select_reduce_fusion
  (101 shorter events, 92.8 us)
Async XLA Ops:
  7.2 566.2 %copy-start = (bf16[1,6144,256]{2,1,0:T(8,128)(2,1)S(1)}, bf16[1,6144,256]{2,1,0:T(8,128)(2,1)}, u32[]{:S(2)}) copy-start(bf16[1,6144,256]{2,1,0:T(8,128)(2,1)} %param.15) | copy-start | bytes 9437188
  7.2 270.1 %all-gather.5.cloned.1.call-start = ((), (), s32[]{:S(2)}) async-start(), calls=%async_computation.5 | async-start | bytes 17694720 | tf_op jit(solution)/shard_map/all_gather | solution.py:92
  61.6 430.6 %all-gather.7.cloned.1.call-start = ((), (), s32[]{:S(2)}) async-start(), calls=%async_computation.6 | async-start | bytes 17694720 | tf_op jit(solution)/shard_map/all_gather | solution.py:71
  77.8 22.1 %copy-start.12 = (bf16[256,2]{0,1:T(2,128)(2,1)S(1)}, bf16[256,2]{0,1:T(2,128)(2,1)}, u32[]{:S(2)}) copy-start(bf16[256,2]{0,1:T(2,128)(2,1)} %param.14) | copy-start | bytes 3076
  99.9 766.5 %all-reduce.4.cloned.1.call-start = ((), (), s32[]{:S(2)}) async-start(), calls=%async_computation.7 | async-start | bytes 15728640
  344.4 9.1 copy-start.8
  344.4 14.6 %copy-start.13 = (bf16[1,256,6144]{2,1,0:T(8,128)(2,1)S(1)}, bf16[1,256,6144]{2,1,0:T(8,128)(2,1)}, u32[]{:S(2)}) copy-start(bf16[1,256,6144]{2,1,0:T(8,128)(2,1)} %param.17) | copy-start | bytes 9437188
  353.5 5.5 copy-start.1
  558.6 8.9 copy-start.7
  567.6 5.8 copy-start.2
  573.4 3.3 copy-start.3
  576.7 3.0 copy-start.9
  576.7 3.3 copy-start.6
  576.7 3.3 copy-start.10
  582.2 7.8 copy-start.4
  582.2 7.8 copy-start.5
  612.0 1.9 copy-start.14
  660.6 249.7 %all-to-all-start.4 = ((bf16[4,1,160]{2,1,0:T(2,128)(2,1)}), bf16[4,1,160]{2,1,0:T(2,128)(2,1)}, u32[]{:S(2)}, u32[]{:S(2)}) async-start(bf16[4,1,160]{2,1,0:T(2,128)(2,1)} %convert_element_type.182), calls=%async_computation.4 | async-start | bytes 8192 | tf_op jit(solution)/shard_map/all_to_all | solution.py:144
  910.3 18.3 %all-to-all-start.3 = ((bf16[4,2,61440]{2,1,0:T(2,128)(2,1)}), bf16[4,2,61440]{2,1,0:T(2,128)(2,1)}, u32[]{:S(2)}, u32[]{:S(2)}) async-start(bf16[4,2,61440]{2,1,0:T(2,128)(2,1)} %reshape.286), calls=%async_computation.3 | async-start | bytes 1966080 | tf_op jit(solution)/shard_map/all_to_all | solution.py:137
  914.8 5.9 copy-start.11
Sparse Core Ops, SparseCore 0:
  61.7 215.5 all-gather.4
  279.5 212.6 all-gather.6
  612.1 254.3 all-reduce.3
where the time goes:
time: 975 us; the launch traced here: 964 us
  waiting for transfers between devices  493 us (51%)
  other arithmetic  167 us (17%)
  local copies, waits for them, and re-layouts  132 us (14%)
  blocking collectives  81.3 us (8%)
  matrix products  67.1 us (7%)
  between operations  14.5 us (1%)
    unnamed x4, waiting for transfers between devices  192 us
    all_gather x1, waiting for transfers between devices, local(): gathered_dy = lax.all_gather(recv_dy[None], 'expert', axis=0, tiled=True)  171 us
    all_gather x1, waiting for transfers between devices, local(): gathered_x = lax.all_gather(recv_x[None], 'expert', axis=0, tiled=True)  130 us
    unnamed x44, local copies, waits for them, and re-layouts  69.8 us
    dot_general x15, matrix products, product(): jnp.einsum(pattern, operand_a, operand_b, preferred_element_type=jnp.floa...  56.2 us
    all_gather x1, other arithmetic, local(): gathered_dy = lax.all_gather(recv_dy[None], 'expert', axis=0, tiled=True)  48 us
    all_gather x1, other arithmetic, local(): gathered_x = lax.all_gather(recv_x[None], 'expert', axis=0, tiled=True)  47.5 us
    psum x1, blocking collectives, local(): lax.psum(back_part.astype(jnp.bfloat16), 'expert').astype(jnp.float32)  38.1 us
  transfers between devices with their start and end apart: 5, of which 4 were waited for; matrix products, arithmetic and copies ran while one was open for 19% of the time, Pallas kernels for 0%

commit v1 on v0

--- a/solution.py
+++ b/solution.py
@@ -1,9 +1,30 @@
+import functools
 import jax
 import jax.numpy as jnp
 from jax import lax
 from jax.sharding import PartitionSpec as P
 
 adapter_scale = 2.0
+
+
+def prepare_page(arr_in, mesh_name):
+    dev_count = jax.lax.psum(1, axis_name=mesh_name)
+    wide_out = arr_in
+    pile = [wide_out]
+    m = 0
+    taken_in = [(jj - 1, jj) for jj in range(1, dev_count)] + [(dev_count - 1, 0)]
+    while m < dev_count - 1:
+        wide_out = jax.lax.ppermute(wide_out, axis_name=mesh_name, perm=taken_in)
+        pile += [wide_out]
+        m += 1
+    return jnp.roll(
+        jnp.concatenate([*reversed(pile)], axis=0),
+        (jax.lax.axis_index(mesh_name) + 1) * wide_out.shape[0],
+        axis=0,
+    )
+
+
+store_desk_on = functools.partial(prepare_page, mesh_name="expert")
 
 
 def product(pattern, operand_a, operand_b):
@@ -89,7 +110,7 @@
     activation = (silu_gate * up_pre).astype(jnp.bfloat16)
     out_part = product("rf,nf->rn", squeeze_local, activation)
     out_low = lax.psum(out_part.astype(jnp.bfloat16), "expert").astype(jnp.float32)
-    gathered_dy = lax.all_gather(recv_dy[None], "expert", axis=0, tiled=True)
+    gathered_dy = store_desk_on(recv_dy[None])
     rows_dy = full_rows(gathered_dy, capacity, part_width)
     back_down = product("nd,fd->nf", rows_dy, down_weight[0])
     back_low = product("rd,nd->rn", spread_local, rows_dy)

time: 975 us -> 957 us (0.982)
  local copies, waits for them, and re-layouts: 132 us -> 185 us
  other arithmetic: 167 us -> 120 us
  blocking collectives: 81.3 us -> 57 us
  starting transfers between devices: 8.42 us -> 18.4 us
    all_gather x1 -> x0, waiting for transfers between devices: 171 us -> none  [local(): gathered_dy = lax.all_gather(recv_dy[None], 'expert', axis=0, tiled=True)]
    ppermute x0 -> x7, waiting for transfers between devices: none -> 144 us  [prepare_page(): wide_out = jax.lax.ppermute(wide_out, axis_name=mesh_name, perm=taken_in)]
    all_gather x1 -> x0, other arithmetic: 48 us -> none  [local(): gathered_dy = lax.all_gather(recv_dy[None], 'expert', axis=0, tiled=True)]
    unnamed x44 -> x85, local copies, waits for them, and re-layouts: 69.8 us -> 98.7 us
    all_to_all x2 -> x0, blocking collectives: 24.3 us -> none  [the longest x1 18.2 us: local(): lax.all_to_all(send_x, 'dp', split_axis=0, concat_axis=0, tiled=True)]
    all_to_all x0 -> x2, waiting for transfers between devices: none -> 13.6 us  [the longest x1 13.6 us: local(): lax.all_to_all(send_x, 'dp', split_axis=0, concat_axis=0, tiled=True)]
    reshape x0 -> x1, local copies, waits for them, and re-layouts: none -> 11.8 us  [full_rows(): gathered.reshape(n_groups, n_sources, capacity, part_width)]
    unnamed x4 -> x3, waiting for transfers between devices: 192 us -> 191 us
  transfers between devices with their start and end apart: 5 -> 13, of which waited for: 4 -> 10; matrix products, arithmetic and copies ran while one was open for 19% -> 19% of each run, Pallas kernels for 0% -> 0%
where the time goes in v1:
time: 957 us; the launch traced here: 946 us
  waiting for transfers between devices  484 us (51%)
  local copies, waits for them, and re-layouts  185 us (19%)
  other arithmetic  120 us (13%)
  matrix products  66.8 us (7%)
  blocking collectives  57 us (6%)
  starting transfers between devices  18.4 us (2%)
  between operations  14.7 us (2%)
    unnamed x3, waiting for transfers between devices  191 us
    ppermute x7, waiting for transfers between devices, prepare_page(): wide_out = jax.lax.ppermute(wide_out, axis_name=mesh_name, perm=taken_in)  144 us
    all_gather x1, waiting for transfers between devices, local(): gathered_x = lax.all_gather(recv_x[None], 'expert', axis=0, tiled=True)  133 us
    unnamed x85, local copies, waits for them, and re-layouts  98.7 us
    dot_general x15, matrix products, product(): jnp.einsum(pattern, operand_a, operand_b, preferred_element_type=jnp.floa...  56 us
    all_gather x1, other arithmetic, local(): gathered_x = lax.all_gather(recv_x[None], 'expert', axis=0, tiled=True)  47.7 us
    psum x1, blocking collectives, local(): lax.psum(back_part.astype(jnp.bfloat16), 'expert').astype(jnp.float32)  38.1 us
    reshape x1, other arithmetic, local(): token_part = lax.psum_scatter(term.reshape(1 * lax.axis_size('expert'), o...  21.8 us
  transfers between devices with their start and end apart: 13, of which 10 were waited for; matrix products, arithmetic and copies ran while one was open for 19% of the time, Pallas kernels for 0%

profile of v1, /device:TPU:0, one launch (start us, length us, event | category | flops | bytes accessed | tf_op | source)
XLA Modules:
  0.0 945.6 jit_solution(10789231666626541868)
XLA Ops:
  26.2 9.3 reduce.13
  38.7 18.9 %all_to_all.38 = bf16[4,2,61440]{2,1,0:T(2,128)(2,1)} all-to-all(bf16[4,2,61440]{2,1,0:T(2,128)(2,1)} %reshape.282), channel_id=1, replica_groups=mesh['dp'=4,'expert'=8] {'dp'}, dimensions={0} | all-to-all | bytes 1966080 | tf_op jit(solution)/shard_map/all_to_all | solution.py:88
  66.7 24.7 %collective-permute-done = bf16[1,4,122880]{2,1,0:T(4,128)(2,1)S(1)} collective-permute-done((bf16[1,4,122880]{2,1,0:T(4,128)(2,1)S(1)}, bf16[1,4,122880]{2,1,0:T(4,128)(2,1)S(1)}, u32[]{:S(2)}, u32[]{:S(2)}) %collective-permute-start) | collective-permute-done | bytes 983072 | tf_op jit(solution)/shard_map/ppermute | solution.py:17
  92.4 25.5 %collective-permute-done.1 = bf16[1,4,122880]{2,1,0:T(4,128)(2,1)S(1)} collective-permute-done((bf16[1,4,122880]{2,1,0:T(4,128)(2,1)S(1)}, bf16[1,4,122880]{2,1,0:T(4,128)(2,1)S(1)}, u32[]{:S(2)}, u32[]{:S(2)}) %collective-permute-start.1) | collective-permute-done | bytes 983072 | tf_op jit(solution)/shard_map/ppermute | solution.py:17
  118.9 24.7 %collective-permute-done.2 = bf16[1,4,122880]{2,1,0:T(4,128)(2,1)S(1)} collective-permute-done((bf16[1,4,122880]{2,1,0:T(4,128)(2,1)S(1)}, bf16[1,4,122880]{2,1,0:T(4,128)(2,1)S(1)}, u32[]{:S(2)}, u32[]{:S(2)}) %collective-permute-start.2) | collective-permute-done | bytes 983072 | tf_op jit(solution)/shard_map/ppermute | solution.py:17
  144.6 23.8 %collective-permute-done.3 = bf16[1,4,122880]{2,1,0:T(4,128)(2,1)S(1)} collective-permute-done((bf16[1,4,122880]{2,1,0:T(4,128)(2,1)S(1)}, bf16[1,4,122880]{2,1,0:T(4,128)(2,1)S(1)}, u32[]{:S(2)}, u32[]{:S(2)}) %collective-permute-start.3) | collective-permute-done | bytes 983072 | tf_op jit(solution)/shard_map/ppermute | solution.py:17
  169.4 23.0 %collective-permute-done.4 = bf16[1,4,122880]{2,1,0:T(4,128)(2,1)S(1)} collective-permute-done((bf16[1,4,122880]{2,1,0:T(4,128)(2,1)S(1)}, bf16[1,4,122880]{2,1,0:T(4,128)(2,1)S(1)}, u32[]{:S(2)}, u32[]{:S(2)}) %collective-permute-start.4) | collective-permute-done | bytes 983072 | tf_op jit(solution)/shard_map/ppermute | solution.py:17
  193.3 22.2 %collective-permute-done.5 = bf16[1,4,122880]{2,1,0:T(4,128)(2,1)} collective-permute-done((bf16[1,4,122880]{2,1,0:T(4,128)(2,1)S(1)}, bf16[1,4,122880]{2,1,0:T(4,128)(2,1)}, u32[]{:S(2)}, u32[]{:S(2)}) %collective-permute-start.5) | collective-permute-done | bytes 983072 | tf_op jit(solution)/shard_map/ppermute | solution.py:17
  223.6 9.3 reduce.14
  240.5 13.6 %all-to-all-done.2 = bf16[4,2,61440]{2,1,0:T(2,128)(2,1)} async-done(((bf16[4,2,61440]{2,1,0:T(2,128)(2,1)}), bf16[4,2,61440]{2,1,0:T(2,128)(2,1)}, u32[]{:S(2)}, u32[]{:S(2)}) %all-to-all-start.2) | async-done | bytes 983072 | tf_op jit(solution)/shard_map/all_to_all | solution.py:87
  289.0 9.1 constant_dynamic-slice_fusion
  298.1 11.8 %reshape.263 = bf16[8,4,160,768]{3,2,1,0:T(8,128)(2,1)} reshape(bf16[8,4,122880]{2,1,0:T(4,128)(2,1)} %constant_dynamic-slice_fusion) | data formatting | bytes 15728640 | tf_op jit(solution)/shard_map/reshape | solution.py:42
  309.9 10.9 %copy.73 = bf16[4,160,8,768]{3,2,1,0:T(8,128)(2,1)} copy(bf16[4,160,8,768]{3,1,0,2:T(8,128)(2,1)} %bitcast.135) | data formatting | bytes 15728640 | tf_op jit(solution)/shard_map/transpose | solution.py:42
  320.9 9.0 copy.91
  329.9 5.5 convolution_bitcast_fusion
  340.1 133.1 %all-gather.3.cloned.1.call-done = bf16[32,1,122880]{2,1,0:T(2,128)(2,1)} async-done(((bf16[4,1,122880]{2,1,0:T(2,128)(2,1)}), bf16[32,1,122880]{2,1,0:T(2,128)(2,1)}) %all-gather.3.cloned.1.call-update) | async-done | bytes 7864336 | tf_op jit(solution)/shard_map/all_gather | solution.py:92
  473.1 47.7 %reduce.2 = bf16[32,122880]{1,0:T(8,128)(2,1)} reduce(bf16[32,1,122880]{2,1,0:T(2,128)(2,1)} %all-gather.3.cloned.1.call-done, bf16[]{:T(256)} %constant.92), dimensions={1}, to_apply=%all-gather.reduce_sub_computation | reduce | bytes 15728642 | tf_op jit(solution)/shard_map/all_gather | solution.py:92
  520.9 8.1 copy.92
  529.0 10.9 %copy.76 = bf16[4,160,8,768]{3,2,1,0:T(8,128)(2,1)} copy(bf16[4,160,8,768]{3,1,0,2:T(8,128)(2,1)} %bitcast.137) | data formatting | bytes 15728640 | tf_op jit(solution)/shard_map/transpose | solution.py:42
  539.9 9.0 copy.93
  548.9 5.8 convolution_convert_fusion.1
  563.0 7.8 fusion.21
  570.8 11.1 %fusion.2 = bf16[1,8,640,768]{3,2,1,0:T(8,128)(2,1)} fusion(f32[640,8,768]{2,0,1:T(8,128)} %fusion.21, bf16[8,768,256]{2,1,0:T(8,128)(2,1)S(1)} %bitcast.139, bf16[640,256]{0,1:T(8,128)(2,1)S(1)} %get-tuple-element.46), kind=kOutput, calls=%fused_computation.7 | convolution fusion | flops 2021130240 | bytes 27066368 | tf_op jit(solution)/shard_map/nf,kdf->knd/dot_general | solution.py:31
  581.9 11.2 %copy.94 = bf16[1,8,640,768]{3,1,2,0:T(8,128)(2,1)} copy(bf16[1,8,640,768]{3,2,1,0:T(8,128)(2,1)} %fusion.2) | data formatting | bytes 15728640
  601.0 38.1 %all-reduce.1 = (bf16[32,640]{1,0:T(8,128)(2,1)S(1)}, bf16[16,640]{1,0:T(8,128)(2,1)S(1)}, bf16[640]{0:T(1024)(128)(2,1)}) all-reduce(bf16[32,640]{1,0:T(8,128)(2,1)} %pad_maximum_fusion.1, bf16[16,640]{1,0:T(8,128)(2,1)} %fusion.15, bf16[640]{0:T(1024)(128)(2,1)} %get-tuple-element.41), channel_id=1, replica_groups=mesh['dp'=4,'expert'=8] {'expert'}, use_global_device_ids=true, to_apply=%region_5.6 | all-reduce | flops 31360 | bytes 125440 | tf_op jit(solution)/shard_map/psum | solution.py:132
  650.4 5.7 fusion
  656.1 191.4 %all-reduce.4.cloned.1.call-done = bf16[8,491520]{1,0:T(8,128)(2,1)} async-done(((bf16[8,491520]{1,0:T(8,128)(2,1)}), bf16[8,491520]{1,0:T(8,128)(2,1)}) %all-reduce.4.cloned.1.call-update) | async-done | bytes 7864336
  847.5 21.8 %fusion.9 = f32[491520]{0:T(1024)} fusion(bf16[8,491520]{1,0:T(8,128)(2,1)} %all-reduce.4.cloned.1.call-done, u32[]{:T(128)} %bitcast.29), kind=kLoop, calls=%fused_computation.16 | loop fusion | flops 491520 | bytes 2949124 | tf_op jit(solution)/shard_map/reshape | solution.py:151
  878.8 9.3 reduce.15
  895.8 5.1 fusion.1
  913.4 8.9 convert_reduce_fusion
  926.5 4.7 gather_fusion
  (157 shorter events, 159.6 us)
Async XLA Ops:
  7.2 547.5 %copy-start = (bf16[1,6144,256]{2,1,0:T(8,128)(2,1)S(1)}, bf16[1,6144,256]{2,1,0:T(8,128)(2,1)}, u32[]{:S(2)}) copy-start(bf16[1,6144,256]{2,1,0:T(8,128)(2,1)} %param.15) | copy-start | bytes 9437188
  22.0 193.6 %copy-start.25 = (bf16[256,2]{0,1:T(2,128)(2,1)S(1)}, bf16[256,2]{0,1:T(2,128)(2,1)}, u32[]{:S(2)}) copy-start(bf16[256,2]{0,1:T(2,128)(2,1)} %param.14) | copy-start | bytes 3076
  64.3 27.1 %collective-permute-start = (bf16[1,4,122880]{2,1,0:T(4,128)(2,1)S(1)}, bf16[1,4,122880]{2,1,0:T(4,128)(2,1)S(1)}, u32[]{:S(2)}, u32[]{:S(2)}) collective-permute-start(bf16[1,4,122880]{2,1,0:T(4,128)(2,1)S(1)} %bitcast.140), channel_id=1, source_target_pairs={{0,1},{1,2},{2,3},{3,4},{4,5},{5,6},{6,7},{7,0},{8,9},{9,10},{10,1... | collective-permute-start | bytes 2949128 | tf_op jit(solution)/shard_map/ppermute | solution.py:17
  92.4 25.5 %collective-permute-start.1 = (bf16[1,4,122880]{2,1,0:T(4,128)(2,1)S(1)}, bf16[1,4,122880]{2,1,0:T(4,128)(2,1)S(1)}, u32[]{:S(2)}, u32[]{:S(2)}) collective-permute-start(bf16[1,4,122880]{2,1,0:T(4,128)(2,1)S(1)} %collective-permute-done), channel_id=1, source_target_pairs={{0,1},{1,2},{2,3},{3,4},{4,5},{5,6},{6,7},{7,0},{8,9},{9,10},{10,1... | collective-permute-start | bytes 2949128 | tf_op jit(solution)/shard_map/ppermute | solution.py:17
  118.9 24.7 %collective-permute-start.2 = (bf16[1,4,122880]{2,1,0:T(4,128)(2,1)S(1)}, bf16[1,4,122880]{2,1,0:T(4,128)(2,1)S(1)}, u32[]{:S(2)}, u32[]{:S(2)}) collective-permute-start(bf16[1,4,122880]{2,1,0:T(4,128)(2,1)S(1)} %collective-permute-done.1), channel_id=1, source_target_pairs={{0,1},{1,2},{2,3},{3,4},{4,5},{5,6},{6,7},{7,0},{8,9},{9,10},{10,1... | collective-permute-start | bytes 2949128 | tf_op jit(solution)/shard_map/ppermute | solution.py:17
  144.6 23.8 %collective-permute-start.3 = (bf16[1,4,122880]{2,1,0:T(4,128)(2,1)S(1)}, bf16[1,4,122880]{2,1,0:T(4,128)(2,1)S(1)}, u32[]{:S(2)}, u32[]{:S(2)}) collective-permute-start(bf16[1,4,122880]{2,1,0:T(4,128)(2,1)S(1)} %collective-permute-done.2), channel_id=1, source_target_pairs={{0,1},{1,2},{2,3},{3,4},{4,5},{5,6},{6,7},{7,0},{8,9},{9,10},{10,1... | collective-permute-start | bytes 2949128 | tf_op jit(solution)/shard_map/ppermute | solution.py:17
  169.4 23.0 %collective-permute-start.4 = (bf16[1,4,122880]{2,1,0:T(4,128)(2,1)S(1)}, bf16[1,4,122880]{2,1,0:T(4,128)(2,1)S(1)}, u32[]{:S(2)}, u32[]{:S(2)}) collective-permute-start(bf16[1,4,122880]{2,1,0:T(4,128)(2,1)S(1)} %collective-permute-done.3), channel_id=1, source_target_pairs={{0,1},{1,2},{2,3},{3,4},{4,5},{5,6},{6,7},{7,0},{8,9},{9,10},{10,1... | collective-permute-start | bytes 2949128 | tf_op jit(solution)/shard_map/ppermute | solution.py:17
  193.3 22.2 %collective-permute-start.5 = (bf16[1,4,122880]{2,1,0:T(4,128)(2,1)S(1)}, bf16[1,4,122880]{2,1,0:T(4,128)(2,1)}, u32[]{:S(2)}, u32[]{:S(2)}) collective-permute-start(bf16[1,4,122880]{2,1,0:T(4,128)(2,1)S(1)} %collective-permute-done.4), channel_id=1, source_target_pairs={{0,1},{1,2},{2,3},{3,4},{4,5},{5,6},{6,7},{7,0},{8,9},{9,10},{10,1... | collective-permute-start | bytes 2949128 | tf_op jit(solution)/shard_map/ppermute | solution.py:17
  215.5 42.8 %collective-permute-start.6 = (bf16[1,4,122880]{2,1,0:T(4,128)(2,1)}, bf16[1,4,122880]{2,1,0:T(4,128)(2,1)}, u32[]{:S(2)}, u32[]{:S(2)}) collective-permute-start(bf16[1,4,122880]{2,1,0:T(4,128)(2,1)} %collective-permute-done.5), channel_id=1, source_target_pairs={{0,1},{1,2},{2,3},{3,4},{4,5},{5,6},{6,7},{7,0},{8,9},{9,10},{10,1... | collective-permute-start | bytes 2949128 | tf_op jit(solution)/shard_map/ppermute | solution.py:17
  216.7 19.4 %all-to-all-start = ((bf16[4,1,160]{2,1,0:T(2,128)(2,1)}), bf16[4,1,160]{2,1,0:T(2,128)(2,1)S(1)}, u32[]{:S(2)}, u32[]{:S(2)}) async-start(bf16[4,1,160]{2,1,0:T(2,128)(2,1)} %convert_element_type.180), calls=%async_computation | async-start | bytes 8192 | tf_op jit(solution)/shard_map/all_to_all | solution.py:89
  236.1 18.0 %all-to-all-start.2 = ((bf16[4,2,61440]{2,1,0:T(2,128)(2,1)}), bf16[4,2,61440]{2,1,0:T(2,128)(2,1)}, u32[]{:S(2)}, u32[]{:S(2)}) async-start(bf16[4,2,61440]{2,1,0:T(2,128)(2,1)} %reshape.280), calls=%async_computation.2 | async-start | bytes 1966080 | tf_op jit(solution)/shard_map/all_to_all | solution.py:87
  240.3 232.8 %all-gather.3.cloned.1.call-start = ((), (), s32[]{:S(2)}) async-start(), calls=%async_computation.5 | async-start | bytes 17694720 | tf_op jit(solution)/shard_map/all_gather | solution.py:92
  258.0 589.4 %all-reduce.4.cloned.1.call-start = ((), (), s32[]{:S(2)}) async-start(), calls=%async_computation.6 | async-start | bytes 15728640
  258.3 10.5 %copy-start.9 = (bf16[1,4,122880]{2,1,0:T(4,128)(2,1)S(1)}, bf16[1,4,122880]{2,1,0:T(4,128)(2,1)}, u32[]{:S(2)}) copy-start(bf16[1,4,122880]{2,1,0:T(4,128)(2,1)} %copy-done.8) | copy-start | bytes 2949124
  258.3 11.8 %copy-start.7 = (bf16[1,4,122880]{2,1,0:T(4,128)(2,1)S(1)}, bf16[1,4,122880]{2,1,0:T(4,128)(2,1)}, u32[]{:S(2)}) copy-start(bf16[1,4,122880]{2,1,0:T(4,128)(2,1)} %copy-done.6) | copy-start | bytes 2949124
  258.3 13.1 %copy-start.5 = (bf16[1,4,122880]{2,1,0:T(4,128)(2,1)S(1)}, bf16[1,4,122880]{2,1,0:T(4,128)(2,1)}, u32[]{:S(2)}) copy-start(bf16[1,4,122880]{2,1,0:T(4,128)(2,1)} %copy-done.4) | copy-start | bytes 2949124
  258.3 14.5 %copy-start.3 = (bf16[4,1,122880]{2,1,0:T(2,128)(2,1)S(1)}, bf16[4,1,122880]{2,1,0:T(2,128)(2,1)}, u32[]{:S(2)}) copy-start(bf16[4,1,122880]{2,1,0:T(2,128)(2,1)} %reshape.283) | copy-start | bytes 2949124
  266.0 14.1 %copy-start.13 = (bf16[1,4,122880]{2,1,0:T(4,128)(2,1)S(1)}, bf16[1,4,122880]{2,1,0:T(4,128)(2,1)}, u32[]{:S(2)}) copy-start(bf16[1,4,122880]{2,1,0:T(4,128)(2,1)} %copy-done.12) | copy-start | bytes 2949124
  268.8 12.7 %copy-start.11 = (bf16[1,4,122880]{2,1,0:T(4,128)(2,1)S(1)}, bf16[1,4,122880]{2,1,0:T(4,128)(2,1)}, u32[]{:S(2)}) copy-start(bf16[1,4,122880]{2,1,0:T(4,128)(2,1)} %copy-done.10) | copy-start | bytes 2949124
  320.9 9.0 copy-start.21
  320.9 14.5 %copy-start.26 = (bf16[1,256,6144]{2,1,0:T(8,128)(2,1)S(1)}, bf16[1,256,6144]{2,1,0:T(8,128)(2,1)}, u32[]{:S(2)}) copy-start(bf16[1,256,6144]{2,1,0:T(8,128)(2,1)} %param.17) | copy-start | bytes 9437188
  329.9 5.5 copy-start.1
  335.4 3.5 copy-start.23
  539.9 9.0 copy-start.20
  548.9 5.8 copy-start.2
  557.8 3.3 copy-start.18
  557.8 3.3 copy-start.19
  563.0 7.8 copy-start.15
  563.0 7.8 copy-start.16
  641.8 249.6 %all-to-all-start.4 = ((bf16[4,1,160]{2,1,0:T(2,128)(2,1)}), bf16[4,1,160]{2,1,0:T(2,128)(2,1)}, u32[]{:S(2)}, u32[]{:S(2)}) async-start(bf16[4,1,160]{2,1,0:T(2,128)(2,1)} %convert_element_type.182), calls=%async_computation.4 | async-start | bytes 8192 | tf_op jit(solution)/shard_map/all_to_all | solution.py:165
  891.3 10.4 %copy-start.24 = (s32[1024]{0:T(1024)S(1)}, s32[1024]{0:T(1024)}, u32[]{:S(2)}) copy-start(s32[1024]{0:T(1024)} %pad_clamp_fusion) | copy-start | bytes 12292
  891.3 18.2 %all-to-all-start.3 = ((bf16[4,2,61440]{2,1,0:T(2,128)(2,1)}), bf16[4,2,61440]{2,1,0:T(2,128)(2,1)}, u32[]{:S(2)}, u32[]{:S(2)}) async-start(bf16[4,2,61440]{2,1,0:T(2,128)(2,1)} %reshape.284), calls=%async_computation.3 | async-start | bytes 1966080 | tf_op jit(solution)/shard_map/all_to_all | solution.py:158
  (9 other events, 13.6 us)
Sparse Core Ops, SparseCore 0:
  258.2 214.9 all-gather.2
  593.2 254.1 all-reduce.3
